TPU v7x, 32 devices: a whole 2x2x4 slice. The times are simulated.
32 devices in a mesh: fsdp: 8 (over z, core), head: 4 (over y, x).
Axes of the slice: x: 2, y: 2, z: 4, core: 2. Of those that a mesh axis runs over, the one named last changes fastest.
Arguments:
- probe_compressed: bfloat16 [2, 32, 1536], P(None, 'fsdp'), may hold values from -6 to 6
- w_uq: bfloat16 [1536, 16384], P('fsdp', 'head'), may hold values from -0.15625 to 0.15625
- w_qr: bfloat16 [1536, 8192], P('fsdp', 'head'), may hold values from -0.15625 to 0.15625
- w_uk: bfloat16 [512, 16384], P('fsdp', 'head'), may hold values from -0.25 to 0.25
- w_uv: bfloat16 [512, 16384], P('fsdp', 'head'), may hold values from -1.5 to 1.5
- cache: bfloat16 [32, 1024, 576], P(('fsdp', 'head')), may hold values from -136 to 136
- new_kv: bfloat16 [2, 32, 576], P(None, ('fsdp', 'head')), may hold values from -6 to 6
- lengths: int32 [32], P(('fsdp', 'head')), may hold values from 1 to 1024
Outputs:
- values: bfloat16 [2, 32, 16384], P(None, 'fsdp', 'head')
All inputs are finite; a program needn't handle non-finite values.
Results may differ from a plain program's by a relative error of at most 0.035.
Values may be sent and summed in bfloat16 or wider, within the bound.
A program may use at most 64 MiB of HBM per device.

v0:
```python
import jax
import jax.numpy as jnp
from jax import lax
from jax.sharding import PartitionSpec as P

NOPE = 128
R = 64
VDIM = 128


def rotate(rope_part, position):
    half = rope_part.shape[-1] // 2
    freqs = 10000.0 ** (-(jnp.arange(half, dtype=jnp.float32) * 2.0 / (2 * half)))
    angle = position[..., None] * freqs
    first = rope_part[..., :half]
    second = rope_part[..., half:]
    cosine_table = jnp.cos(angle)
    sine = jnp.sin(angle)
    return jnp.concatenate(
        [first * cosine_table - second * sine, first * sine + second * cosine_table], axis=-1
    )


def attend(query, keys, fresh, extent):
    steps = query.shape[0]
    heads = query.shape[1]
    width = keys.shape[1]
    latent_width = width - R
    position = (extent + jnp.arange(steps, dtype=jnp.int32)).astype(jnp.float32)
    rotated = rotate(query[:, :, latent_width:].astype(jnp.float32), position[:, None])
    joined = jnp.concatenate([query[:, :, :latent_width], rotated.astype(jnp.bfloat16)], axis=2)
    joined = joined.reshape(steps * heads, width)
    factor = (NOPE + R) ** (-0.5)
    older = jnp.dot(joined, keys.T, preferred_element_type=jnp.float32) * factor
    valid = jnp.arange(keys.shape[0], dtype=jnp.int32) < extent
    older = jnp.where(valid[None, :], older, -1e30)
    newer = jnp.dot(joined, fresh.T, preferred_element_type=jnp.float32) * factor
    order = jnp.arange(steps, dtype=jnp.int32)
    allowed = jnp.repeat(order[None, :] <= order[:, None], heads, axis=0)
    newer = jnp.where(allowed, newer, -1e30)
    highest = jnp.maximum(jnp.max(older, axis=1), jnp.max(newer, axis=1))
    weight_old = jnp.exp(older - highest[:, None])
    weight_new = jnp.exp(newer - highest[:, None])
    total = jnp.sum(weight_old, axis=1) + jnp.sum(weight_new, axis=1)
    mixed = jnp.dot(
        weight_old.astype(jnp.bfloat16), keys[:, :latent_width], preferred_element_type=jnp.float32
    )
    mixed = mixed + jnp.dot(
        weight_new.astype(jnp.bfloat16), fresh[:, :latent_width], preferred_element_type=jnp.float32
    )
    return (mixed / total[:, None]).astype(jnp.bfloat16).reshape(steps, heads, latent_width)


def per_device(probe_compressed, w_uq, w_qr, w_uk, w_uv, cache, new_kv, lengths):
    heads = w_uk.shape[1] // NOPE
    steps, group, rank = probe_compressed.shape
    flattened = probe_compressed.reshape(steps * group, rank)
    key_up, value_up, rotary_up_weight = (
        lax.all_gather(w_uk, "fsdp", axis=0, tiled=True),
        lax.all_gather(w_uv, "fsdp", axis=0, tiled=True),
        lax.all_gather(w_qr, "fsdp", axis=0, tiled=True),
    )
    key_heads = key_up.reshape(key_up.shape[0], heads, NOPE)
    slab = lax.all_gather(w_uq, "fsdp", axis=0, tiled=True)
    count = slab.shape[0]
    slab_heads = slab.reshape(count, heads, NOPE)
    absorbed = jnp.einsum("rhn,chn->hrc", slab_heads, key_heads, preferred_element_type=jnp.float32)
    absorbed = absorbed.astype(jnp.bfloat16)
    summed = jnp.einsum("qr,hrc->qhc", flattened, absorbed, preferred_element_type=jnp.float32)
    latent = summed.astype(jnp.bfloat16)
    latent_rank = key_up.shape[0]
    rope_query = jnp.dot(flattened, rotary_up_weight, preferred_element_type=jnp.float32).astype(
        jnp.bfloat16
    )
    rope_query = rope_query.reshape(steps * group, heads, R)
    query_matrix = jnp.concatenate([latent, rope_query], axis=2).reshape(
        steps, group, heads, latent_rank + R
    )
    row_queries = lax.all_to_all(query_matrix, "head", split_axis=1, concat_axis=2, tiled=True)
    mixed = jax.vmap(attend, in_axes=(1, 0, 1, 0), out_axes=1)(row_queries, cache, new_kv, lengths)
    combined_across_heads = lax.all_to_all(mixed, "head", split_axis=2, concat_axis=1, tiled=True)
    value_heads = value_up.reshape(latent_rank, heads, VDIM)
    attention_output = jnp.einsum(
        "sghc,chv->sghv", combined_across_heads, value_heads, preferred_element_type=jnp.float32
    )
    return attention_output.astype(jnp.bfloat16).reshape(steps, group, heads * VDIM)


def solution(mesh):
    in_specs = (
        P(None, "fsdp", None),
        P("fsdp", "head"),
        P("fsdp", "head"),
        P("fsdp", "head"),
        P("fsdp", "head"),
        P(("fsdp", "head"), None, None),
        P(None, ("fsdp", "head"), None),
        P(("fsdp", "head")),
    )
    out_specs = P(None, "fsdp", "head")
    return jax.shard_map(
        per_device, mesh=mesh, in_specs=in_specs, out_specs=out_specs, check_vma=False
    )
```

profile of v0, /device:TPU:7, one launch (start us, length us, event | category | flops | bytes accessed | tf_op | source)
XLA Modules:
  0.0 315.3 jit_solution(7329103824131219644)
XLA Ops:
  6.5 0.0 all-gather.7.cloned.1.call-start
  6.5 0.7 all-gather.7.cloned.1.call-update
  7.3 0.0 all-gather.9.cloned.1.call-start
  7.3 0.7 all-gather.9.cloned.1.call-update
  8.0 0.0 all-gather.5.cloned.1.call-start
  8.1 0.7 all-gather.5.cloned.1.call-update
  8.7 0.0 all-gather.11.cloned.1.call-start
  8.8 0.5 all-gather.11.cloned.1.call-update
  9.3 0.8 reshape.301
  10.1 0.8 reshape.292
  11.5 0.1 multiply_cosine_fusion
  11.6 45.8 %all-gather.7.cloned.1.call-done = bf16[512,4096]{1,0:T(8,128)(2,1)} async-done(((bf16[64,4096]{1,0:T(8,128)(2,1)}), bf16[512,4096]{1,0:T(8,128)(2,1)}) %all-gather.7.cloned.1.call-update) | async-done | bytes 4194320 | tf_op jit(solution)/shard_map/all_gather | solution.py:59
  57.4 6.5 %copy.38 = bf16[512,4096]{0,1:T(8,128)(2,1)} copy(bf16[512,4096]{1,0:T(8,128)(2,1)} %all-gather.7.cloned.1.call-done) | data formatting | bytes 8388608 | tf_op jit(solution)/shard_map/all_gather | solution.py:59
  63.9 58.7 %all-gather.9.cloned.1.call-done = bf16[1536,2048]{1,0:T(8,128)(2,1)} async-done(((bf16[192,2048]{1,0:T(8,128)(2,1)}), bf16[1536,2048]{1,0:T(8,128)(2,1)}) %all-gather.9.cloned.1.call-update) | async-done | bytes 6291472 | tf_op jit(solution)/shard_map/all_gather | solution.py:61
  122.6 3.7 %convolution_convert_fusion = bf16[8,2048]{1,0:T(8,128)(2,1)S(1)} fusion(bf16[8,1536]{1,0:T(8,128)(2,1)S(1)} %reshape.292, bf16[1536,2048]{1,0:T(8,128)(2,1)} %all-gather.9.cloned.1.call-done), kind=kOutput, calls=%fused_computation.3 | convolution fusion | flops 50348032 | bytes 6348800 | tf_op jit(solution)/shard_map/dot_general | solution.py:72
  126.3 0.1 concatenate.31
  126.4 113.2 %all-gather.5.cloned.1.call-done = bf16[1536,4096]{1,0:T(8,128)(2,1)} async-done(((bf16[192,4096]{1,0:T(8,128)(2,1)}), bf16[1536,4096]{1,0:T(8,128)(2,1)}) %all-gather.5.cloned.1.call-update) | async-done | bytes 12582928 | tf_op jit(solution)/shard_map/all_gather | solution.py:64
  239.6 16.8 %copy.37 = bf16[1536,4096]{0,1:T(8,128)(2,1)} copy(bf16[1536,4096]{1,0:T(8,128)(2,1)} %all-gather.5.cloned.1.call-done) | data formatting | bytes 25165824 | tf_op jit(solution)/shard_map/all_gather | solution.py:64
  256.4 25.0 %fusion.11 = bf16[8,32,512]{2,0,1:T(8,128)(2,1)S(1)} fusion(bf16[8,1536,1]{1,0,2:T(8,128)(2,1)S(1)} %reshape.301, bf16[1536,32,128]{0,2,1:T(8,128)(2,1)} %bitcast.89, bf16[512,32,128]{0,2,1:T(8,128)(2,1)} %bitcast.90), kind=kOutput, calls=%fused_computation.11 | convolution fusion | flops 6870401024 | bytes 17063936 | tf_op jit(solution)/shard_map/qr,hrc->qhc/dot_general | solution.py:69
  281.4 0.0 copy-start
  281.4 0.0 copy-start.1
  281.4 0.1 concatenate.30
  281.5 0.1 copy.41
  281.6 0.8 pad_maximum_fusion
  282.3 3.7 %all-to-all-start = ((bf16[2,4,32,576]{3,2,0,1:T(8,128)(2,1)}), bf16[2,4,32,576]{3,2,0,1:T(8,128)(2,1)S(1)}, u32[]{:S(2)}, u32[]{:S(2)}) async-start(bf16[2,4,32,576]{3,2,0,1:T(8,128)(2,1)} %pad_maximum_fusion), calls=%async_computation | async-start | bytes 655360 | tf_op jit(solution)/shard_map/all_to_all | solution.py:79
  286.0 0.1 broadcast_bitcast_fusion
  286.1 4.3 %all-to-all-done = bf16[2,4,32,576]{3,2,0,1:T(8,128)(2,1)S(1)} async-done(((bf16[2,4,32,576]{3,2,0,1:T(8,128)(2,1)}), bf16[2,4,32,576]{3,2,0,1:T(8,128)(2,1)S(1)}, u32[]{:S(2)}, u32[]{:S(2)}) %all-to-all-start) | async-done | bytes 294944 | tf_op jit(solution)/shard_map/all_to_all | solution.py:79
  290.5 0.1 fusion.37
  290.6 0.0 copy-done
  290.6 0.2 fusion.39
  290.9 0.0 copy-done.1
  290.9 0.7 fusion.38
  291.6 0.3 fusion.18
  291.9 0.3 fusion.28
  292.2 0.5 fusion.6
  292.7 1.0 copy.44
  293.7 4.5 %all-to-all-start.1 = ((bf16[2,1,128,512]{3,0,1,2:T(2,128)(2,1)}), bf16[2,1,128,512]{3,0,1,2:T(2,128)(2,1)S(1)}, u32[]{:S(2)}, u32[]{:S(2)}) async-start(bf16[2,1,128,512]{3,0,1,2:T(2,128)(2,1)} %copy.44), calls=%async_computation.1 | async-start | bytes 524288 | tf_op jit(solution)/shard_map/all_to_all | solution.py:81
  298.2 0.0 all-gather.11.cloned.1.call-done
  298.2 6.5 %copy.46 = bf16[512,4096]{0,1:T(8,128)(2,1)} copy(bf16[512,4096]{1,0:T(8,128)(2,1)} %all-gather.11.cloned.1.call-done) | data formatting | bytes 8388608 | tf_op jit(solution)/shard_map/all_gather | solution.py:60
  304.7 0.0 all-to-all-done.1
  304.7 3.4 %fusion.14 = bf16[32,2,1,4,128]{4,3,2,1,0:T(4,128)(2,1)S(1)} fusion(bf16[512,32,128,1]{0,2,3,1:T(8,128)(2,1)} %bitcast.88, bf16[2,4,32,512]{3,0,2,1:T(2,128)(2,1)S(1)} %bitcast.93), kind=kOutput, calls=%fused_computation.13 | convolution fusion | flops 33587200 | bytes 4521984 | tf_op jit(solution)/shard_map/sghc,chv->sghv/dot_general | solution.py:83
  308.1 0.7 copy.65
  (11 shorter events, 0.2 us)
Async XLA Ops:
  6.5 50.9 %all-gather.7.cloned.1.call-start = ((), (), s32[]{:S(2)}) async-start(), calls=%async_computation.3 | async-start | bytes 4718592 | tf_op jit(solution)/shard_map/all_gather | solution.py:59
  7.3 115.3 %all-gather.9.cloned.1.call-start = ((), (), s32[]{:S(2)}) async-start(), calls=%async_computation.4 | async-start | bytes 7077888 | tf_op jit(solution)/shard_map/all_gather | solution.py:61
  8.0 231.6 %all-gather.5.cloned.1.call-start = ((), (), s32[]{:S(2)}) async-start(), calls=%async_computation.2 | async-start | bytes 14155776 | tf_op jit(solution)/shard_map/all_gather | solution.py:64
  8.7 289.5 %all-gather.11.cloned.1.call-start = ((), (), s32[]{:S(2)}) async-start(), calls=%async_computation.5 | async-start | bytes 4718592 | tf_op jit(solution)/shard_map/all_gather | solution.py:60
  281.4 9.2 %copy-start = (bf16[2,1,576]{2,0,1:T(2,128)(2,1)S(1)}, bf16[2,1,576]{2,0,1:T(2,128)(2,1)}, u32[]{:S(2)}) copy-start(bf16[2,1,576]{2,0,1:T(2,128)(2,1)} %param.14) | copy-start | bytes 6916
  281.4 9.5 %copy-start.1 = (bf16[1,1024,576]{1,2,0:T(8,128)(2,1)S(1)}, bf16[1,1024,576]{1,2,0:T(8,128)(2,1)}, u32[]{:S(2)}) copy-start(bf16[1,1024,576]{1,2,0:T(8,128)(2,1)} %param.13) | copy-start | bytes 3538948
  282.3 8.1 %all-to-all-start = ((bf16[2,4,32,576]{3,2,0,1:T(8,128)(2,1)}), bf16[2,4,32,576]{3,2,0,1:T(8,128)(2,1)S(1)}, u32[]{:S(2)}, u32[]{:S(2)}) async-start(bf16[2,4,32,576]{3,2,0,1:T(8,128)(2,1)} %pad_maximum_fusion), calls=%async_computation | async-start | bytes 655360 | tf_op jit(solution)/shard_map/all_to_all | solution.py:79
  293.7 11.0 %all-to-all-start.1 = ((bf16[2,1,128,512]{3,0,1,2:T(2,128)(2,1)}), bf16[2,1,128,512]{3,0,1,2:T(2,128)(2,1)S(1)}, u32[]{:S(2)}, u32[]{:S(2)}) async-start(bf16[2,1,128,512]{3,0,1,2:T(2,128)(2,1)} %copy.44), calls=%async_computation.1 | async-start | bytes 524288 | tf_op jit(solution)/shard_map/all_to_all | solution.py:81
Sparse Core Ops, SparseCore 0:
  8.9 48.4 all-gather.6
  59.0 63.4 all-gather.8
  124.2 115.3 all-gather.4
  241.1 45.0 all-gather.10
where the time goes:
time: 318 us; the launch traced here: 315 us
  waiting for transfers between devices  225 us (71%)
  matrix products  33.8 us (11%)
  local copies, waits for them, and re-layouts  33.4 us (11%)
  between operations  13.9 us (4%)
  starting transfers between devices  8.33 us (3%)
    all_gather x1, waiting for transfers between devices, per_device(): slab = lax.all_gather(w_uq, 'fsdp', axis=0, tiled=True)  113 us
    all_gather x1, waiting for transfers between devices, per_device(): lax.all_gather(w_qr, 'fsdp', axis=0, tiled=True)  58.7 us
    all_gather x1, waiting for transfers between devices, per_device(): lax.all_gather(w_uk, 'fsdp', axis=0, tiled=True)  45.8 us
    dot_general x1, matrix products, per_device(): jnp.einsum('qr,hrc->qhc', flattened, absorbed, preferred_element_type=jnp...  25 us
    all_gather x1, local copies, waits for them, and re-layouts, per_device(): slab = lax.all_gather(w_uq, 'fsdp', axis=0, tiled=True)  16.8 us
    all_gather x1, local copies, waits for them, and re-layouts, per_device(): lax.all_gather(w_uk, 'fsdp', axis=0, tiled=True)  6.49 us
    all_gather x1, local copies, waits for them, and re-layouts, per_device(): lax.all_gather(w_uv, 'fsdp', axis=0, tiled=True)  6.47 us
  transfers between devices with their start and end apart: 6, of which 4 were waited for; matrix products, arithmetic and copies ran while one was open for 20% of the time, Pallas kernels for 0%

commit v1 on v0

--- a/solution.py
+++ b/solution.py
@@ -1,6 +1,11 @@
+import functools
+
 import jax
 import jax.numpy as jnp
+import numpy as np
 from jax import lax
+from jax.experimental import pallas as pl
+from jax.experimental.pallas import tpu as pltpu
 from jax.sharding import PartitionSpec as P
 
 NOPE = 128
@@ -86,6 +91,355 @@
     return attention_output.astype(jnp.bfloat16).reshape(steps, group, heads * VDIM)
 
 
+def fused(F, G, steps, own,
+          len_ref, freq_ref, probe_ref, new_ref, uq_hbm, qr_hbm, uk_hbm, uv_hbm, cache_hbm,
+          out_ref,
+          uq, wqr, wk, wv, kv, ps, pr, pp, pv, zs, zr, qs, qr, ms, mr, os_, or_,
+          lsem, sp, rp, sk, rk, sv, rv, spp, rpp, sz, rz, sq, rq, sm, rm, so, ro):
+    f32, bf16 = jnp.float32, jnp.bfloat16
+    f = lax.axis_index("fsdp")
+    hd = lax.axis_index("head")
+    N = F * G
+    Z = F // 2
+    me = f * G + hd
+    z, core = lax.div(f, 2), lax.rem(f, 2)
+    ck = uk_hbm.shape[0]
+    cols = own * NOPE
+    rcols = own * R
+    C = ck * F
+    stored = cache_hbm.shape[1]
+    slice_rank = uq.shape[0]
+    per = steps * own
+    queries = F * steps * G
+    expanded = N * per
+
+    def rcopy(src, dst, ssem, rsem, ff, hh):
+        return pltpu.make_async_remote_copy(
+            src_ref=src, dst_ref=dst, send_sem=ssem, recv_sem=rsem,
+            device_id={"fsdp": ff, "head": hh}, device_id_type=pl.DeviceIdType.MESH,
+        )
+
+    def block(t, width):
+        return pl.ds(pl.multiple_of(t * width, 128), width)
+
+    mine = pl.ds(pl.multiple_of(f * ck, 16), ck)
+    load_uq = pltpu.make_async_copy(uq_hbm, uq, lsem.at[0])
+    load_qr = pltpu.make_async_copy(qr_hbm, wqr, lsem.at[1])
+    load_kv = pltpu.make_async_copy(cache_hbm.at[0], kv.at[pl.ds(0, stored)], lsem.at[2])
+    load_uk = pltpu.make_async_copy(uk_hbm.at[:, block(f, cols)], wk.at[mine], lsem.at[3])
+    load_uv = pltpu.make_async_copy(uv_hbm.at[:, block(f, cols)], wv.at[mine], lsem.at[4])
+    loads = [load_uq, load_qr, load_kv, load_uk, load_uv]
+    for c in loads:
+        c.start()
+
+    bar = pltpu.get_barrier_semaphore()
+
+    def greet(k, carry):
+        t = lax.rem(me + k, N)
+        pl.semaphore_signal(
+            bar, inc=1, device_id={"fsdp": lax.div(t, G), "head": lax.rem(t, G)},
+            device_id_type=pl.DeviceIdType.MESH,
+        )
+        return carry
+
+    lax.fori_loop(1, N, greet, 0)
+
+    probe8 = jnp.concatenate([probe_ref[s].astype(f32) for s in range(steps)], axis=0)
+    for p in range(F):
+        ps[p] = probe8[:, p * slice_rank:(p + 1) * slice_rank].astype(bf16)
+    pr[pl.ds(f, 1)] = ps[pl.ds(f, 1)]
+
+    pl.semaphore_wait(bar, N - 1)
+
+    def probe_copy(k):
+        t = lax.rem(f + k, F)
+        return rcopy(ps.at[t], pr.at[f], sp.at[k], rp.at[f], t, hd)
+
+    def uk_copy(k):
+        t = lax.rem(f + k, F)
+        return rcopy(uk_hbm.at[:, block(t, cols)], wk.at[mine], sk.at[k], rk.at[f], t, hd)
+
+    def uv_copy(k):
+        t = lax.rem(f + k, F)
+        return rcopy(uv_hbm.at[:, block(t, cols)], wv.at[mine], sv.at[k], rv.at[f], t, hd)
+
+    def each(first, last, make, method):
+        def step(k, carry):
+            getattr(make(k), method)()
+            return carry
+        lax.fori_loop(first, last, step, 0)
+
+    each(1, F, probe_copy, "start")
+    each(1, F, uk_copy, "start")
+
+    tail = kv.shape[0] - stored
+    at = lax.broadcasted_iota(jnp.int32, (tail, kv.shape[1]), 0)
+    fill = jnp.zeros((tail, kv.shape[1]), f32)
+    for s in range(steps):
+        fill = jnp.where(at == s, new_ref[s].astype(f32), fill)
+    kv[stored:stored + tail, :] = fill.astype(bf16)
+
+    row8 = lax.broadcasted_iota(jnp.int32, (per, 128), 0)
+    step8 = lax.div(row8, own)
+    angle = (len_ref[0] + step8).astype(f32) * freq_ref[...]
+    cos8, sin8 = jnp.cos(angle), jnp.sin(angle)
+
+    load_uq.wait()
+    load_qr.wait()
+
+    def probe_arrival(k, carry):
+        src = lax.rem(f + k, F)
+        rcopy(ps.at[src], pr.at[src], sp.at[k], rp.at[src], src, hd).wait_recv()
+        return carry
+
+    lax.fori_loop(1, F, probe_arrival, 0)
+    probes = pr[...].astype(f32).reshape(queries, slice_rank).astype(bf16)
+
+    def partial_of(t):
+        a = jnp.dot(probes, uq[:, block(t, cols)], preferred_element_type=f32)
+        b = jnp.dot(probes, wqr[:, block(t, rcols)], preferred_element_type=f32)
+        return a, b
+
+    def pair_copy(k):
+        zz = lax.rem(z + k, Z)
+        return rcopy(pp.at[zz], pv.at[zz], spp.at[zz], rpp.at[zz], z * 2 + 1 - core, hd)
+
+    def to_partner(k, carry):
+        zz = lax.rem(z + k, Z)
+        a, b = partial_of(zz * 2 + 1 - core)
+        pp[zz, :, 0:cols] = a.astype(bf16)
+        pp[zz, :, cols:cols + rcols] = b.astype(bf16)
+        pair_copy(k).start()
+        return carry
+
+    lax.fori_loop(1, Z + 1, to_partner, 0)
+
+    def line_copy(k):
+        zz = lax.rem(z + k, Z)
+        return rcopy(zs.at[zz], zr.at[z], sz.at[zz], rz.at[z], zz * 2 + core, hd)
+
+    def along_line(k, carry):
+        zz = lax.rem(z + k, Z)
+        a, b = partial_of(zz * 2 + core)
+        pair_copy(k).wait_recv()
+        zs[zz, :, 0:cols] = (a + pv[zz, :, 0:cols].astype(f32)).astype(bf16)
+        zs[zz, :, cols:cols + rcols] = (b + pv[zz, :, cols:cols + rcols].astype(f32)).astype(bf16)
+        line_copy(k).start()
+        return carry
+
+    lax.fori_loop(1, Z, along_line, 0)
+    a, b = partial_of(f)
+    pair_copy(0).wait_recv()
+    nope = a + pv[z, :, 0:cols].astype(f32)
+    rope = b + pv[z, :, cols:cols + rcols].astype(f32)
+    for k in range(1, Z):
+        src = lax.rem(z + k, Z)
+        rcopy(zs.at[src], zr.at[src], sz.at[src], rz.at[src], src * 2 + core, hd).wait_recv()
+        nope = nope + zr[src, :, 0:cols].astype(f32)
+        rope = rope + zr[src, :, cols:cols + rcols].astype(f32)
+    nope = nope.astype(bf16)
+    rope = rope.astype(bf16)
+
+    def iota(shape, axis):
+        return lax.broadcasted_iota(jnp.int32, shape, axis)
+
+    er = iota((expanded, queries), 0)
+    ed = lax.div(er, per)
+    es = lax.div(lax.rem(er, per), own)
+    pick = (lax.div(ed, G) * (steps * G) + es * G + lax.rem(ed, G)) == iota((expanded, queries), 1)
+    pick = jnp.where(pick, 1.0, 0.0).astype(bf16)
+    head_of_row = lax.rem(iota((expanded, cols), 0), own)
+    own_head = lax.div(iota((expanded, cols), 1), NOPE) == head_of_row
+    own_rope = lax.div(iota((expanded, rcols), 1), R) == lax.rem(iota((expanded, rcols), 0), own)
+    fold = lax.rem(iota((rcols, 128), 0), R) == iota((rcols, 128), 1)
+    fold = jnp.where(fold, 1.0, 0.0).astype(bf16)
+    wide = jnp.where(own_head, jnp.dot(pick, nope, preferred_element_type=f32), 0.0).astype(bf16)
+    wide_rope = jnp.where(own_rope, jnp.dot(pick, rope, preferred_element_type=f32), 0.0).astype(bf16)
+    rope_rows = jnp.dot(wide_rope, fold, preferred_element_type=f32)
+
+    load_uk.wait()
+
+    def weight_arrival(hbm, w, ssem, rsem):
+        def step(k, carry):
+            src = lax.rem(f + k, F)
+            there = pl.ds(pl.multiple_of(src * ck, 16), ck)
+            rcopy(hbm.at[:, block(src, cols)], w.at[there], ssem.at[k], rsem.at[src], src, hd).wait_recv()
+            return carry
+        lax.fori_loop(1, F, step, 0)
+
+    weight_arrival(uk_hbm, wk, sk, rk)
+    latent = lax.dot_general(wide, wk[...], (((1,), (1,)), ((), ())), preferred_element_type=f32)
+    qs[:, :, 0:C] = latent.reshape(N, per, C).astype(bf16)
+    qs[:, :, C:C + 128] = rope_rows.reshape(N, per, 128).astype(bf16)
+
+    def query_copy(k):
+        t = lax.rem(me + k, N)
+        return rcopy(qs.at[t], qr.at[me], sq.at[k], rq.at[me], lax.div(t, G), lax.rem(t, G))
+
+    each(1, N, query_copy, "start")
+    each(1, F, uv_copy, "start")
+    qr[pl.ds(me, 1)] = qs[pl.ds(me, 1)]
+
+    load_kv.wait()
+    factor = (NOPE + R) ** -0.5
+    chunk = F
+    sr = iota((128, 128), 0)
+    sc = iota((128, 128), 1)
+    half = R // 2
+    swap = jnp.where((sr == sc + half) & (sc < half), -1.0, 0.0)
+    swap = swap + jnp.where((sr == sc - half) & (sc >= half) & (sc < R), 1.0, 0.0)
+    swap = swap.astype(bf16)
+    rows = chunk * per
+    keys = kv.shape[0]
+    cosines = jnp.broadcast_to(cos8[None], (chunk, per, 128)).reshape(rows, 128)
+    sines = jnp.broadcast_to(sin8[None], (chunk, per, 128)).reshape(rows, 128)
+    column = iota((rows, keys), 1)
+    step_of = lax.div(lax.rem(iota((rows, keys), 0), per), own)
+    shown = (column < len_ref[0]) | ((column >= stored) & (column <= stored + step_of))
+
+    def mixed_copy(e):
+        return rcopy(ms.at[e], mr.at[me], sm.at[e], rm.at[me], lax.div(e, G), lax.rem(e, G))
+
+    def attend_chunk(b, carry):
+        base = b * chunk
+
+        def arrival(i, c):
+            src = base + i
+
+            @pl.when(src != me)
+            def _():
+                rcopy(qs.at[src], qr.at[src], sq.at[0], rq.at[src], lax.div(src, G), lax.rem(src, G)).wait_recv()
+            return c
+
+        lax.fori_loop(0, chunk, arrival, 0)
+        x = qr[pl.ds(base, chunk)].astype(f32).reshape(rows, C + 128)
+        lat = x[:, 0:C].astype(bf16)
+        xr = x[:, C:C + 128]
+        turned = jnp.dot(xr.astype(bf16), swap, preferred_element_type=f32)
+        rot = (xr * cosines + turned * sines).astype(bf16)[:, 0:R]
+        nt = (((1,), (1,)), ((), ()))
+        s = lax.dot_general(lat, kv[:, 0:C], nt, preferred_element_type=f32)
+        s = s + lax.dot_general(rot, kv[:, C:C + R], nt, preferred_element_type=f32)
+        s = jnp.where(shown, s * factor, -1e30)
+        m = jnp.max(s, axis=1, keepdims=True)
+        w = jnp.exp(s - m)
+        total = jnp.sum(w, axis=1, keepdims=True)
+        mix = jnp.dot(w.astype(bf16), kv[:, 0:C], preferred_element_type=f32) / total
+        ms[pl.ds(base, chunk)] = mix.reshape(chunk, per, C).astype(bf16)
+
+        def send(i, c):
+            e = base + i
+
+            @pl.when(e != me)
+            def _():
+                mixed_copy(e).start()
+            return c
+
+        lax.fori_loop(0, chunk, send, 0)
+        return carry
+
+    lax.fori_loop(0, N // chunk, attend_chunk, 0)
+    mr[pl.ds(me, 1)] = ms[pl.ds(me, 1)]
+
+    load_uv.wait()
+    weight_arrival(uv_hbm, wv, sv, rv)
+
+    def mixed_arrival(k, carry):
+        src = lax.rem(me + k, N)
+        rcopy(ms.at[src], mr.at[src], sm.at[src], rm.at[src], lax.div(src, G), lax.rem(src, G)).wait_recv()
+        return carry
+
+    lax.fori_loop(1, N, mixed_arrival, 0)
+    mixed = mr[...].astype(f32).reshape(expanded, C).astype(bf16)
+    values = jnp.dot(mixed, wv[...], preferred_element_type=f32)
+    values = jnp.where(own_head, values, 0.0).astype(bf16)
+    values = lax.dot_general(pick, values, (((0,), (0,)), ((), ())), preferred_element_type=f32)
+    os_[...] = values.reshape(F, steps * G, cols).astype(bf16)
+
+    def out_copy(k):
+        t = lax.rem(f + k, F)
+        return rcopy(os_.at[t], or_.at[f], so.at[k], ro.at[f], t, hd)
+
+    each(1, F, out_copy, "start")
+    or_[pl.ds(f, 1)] = os_[pl.ds(f, 1)]
+
+    def out_arrival(k, carry):
+        src = lax.rem(f + k, F)
+        rcopy(os_.at[src], or_.at[src], so.at[k], ro.at[src], src, hd).wait_recv()
+        return carry
+
+    lax.fori_loop(1, F, out_arrival, 0)
+    for p in range(F):
+        v = or_[p].astype(f32)
+        for s in range(steps):
+            out_ref[s, :, p * cols:(p + 1) * cols] = v[s * G:(s + 1) * G].astype(bf16)
+
+    each(1, F, probe_copy, "wait_send")
+    each(1, F, uk_copy, "wait_send")
+    each(1, F, uv_copy, "wait_send")
+    each(1, Z + 1, pair_copy, "wait_send")
+    each(1, Z, line_copy, "wait_send")
+    each(1, N, query_copy, "wait_send")
+    each(1, F, out_copy, "wait_send")
+
+    def mixed_sent(k, carry):
+        mixed_copy(lax.rem(me + k, N)).wait_send()
+        return carry
+
+    lax.fori_loop(1, N, mixed_sent, 0)
+
+
+def one_kernel(probe_compressed, w_uq, w_qr, w_uk, w_uv, cache, new_kv, lengths):
+    F, G = lax.axis_size("fsdp"), lax.axis_size("head")
+    N, Z = F * G, F // 2
+    steps, group, _ = probe_compressed.shape
+    ck, heads = w_uk.shape[0], w_uk.shape[1] // NOPE
+    own = heads // F
+    C = ck * F
+    queries = F * steps * G
+    per = steps * own
+    cols, rcols = own * NOPE, own * R
+    stored, width = cache.shape[1:]
+    half = R // 2
+    freqs = 10000.0 ** (-(np.arange(half, dtype=np.float32) * 2.0 / R))
+    freqs = np.concatenate([freqs, freqs, np.zeros(128 - R)]).astype(np.float32)[None]
+    bf16 = jnp.bfloat16
+    vm = lambda *shape: pltpu.VMEM(shape, bf16)
+    dma = lambda n: pltpu.SemaphoreType.DMA((n,))
+    vmem = pl.BlockSpec(memory_space=pltpu.VMEM)
+    hbm = pl.BlockSpec(memory_space=pl.ANY)
+    return pl.pallas_call(
+        functools.partial(fused, F, G, steps, own),
+        out_shape=jax.ShapeDtypeStruct((steps, group, heads * VDIM), bf16),
+        in_specs=[pl.BlockSpec(memory_space=pltpu.SMEM), vmem, vmem, vmem, hbm, hbm, hbm, hbm, hbm],
+        out_specs=vmem,
+        scratch_shapes=[
+            vm(*w_uq.shape), vm(*w_qr.shape), vm(C, cols), vm(C, cols), vm(stored + 128, width),
+            vm(F, steps * G, w_uq.shape[0]), vm(F, steps * G, w_uq.shape[0]),
+            vm(Z, queries, cols + rcols), vm(Z, queries, cols + rcols),
+            vm(Z, queries, cols + rcols), vm(Z, queries, cols + rcols),
+            vm(N, per, C + 128), vm(N, per, C + 128), vm(N, per, C), vm(N, per, C),
+            vm(F, steps * G, cols), vm(F, steps * G, cols),
+            dma(5), dma(F), dma(F), dma(F), dma(F), dma(F), dma(F), dma(Z), dma(Z), dma(Z), dma(Z),
+            dma(N), dma(N), dma(N), dma(N), dma(F), dma(F),
+        ],
+        compiler_params=pltpu.CompilerParams(
+            collective_id=0, has_side_effects=True, vmem_limit_bytes=48 * 2**20
+        ),
+    )(lengths, jnp.asarray(freqs), probe_compressed, new_kv, w_uq, w_qr, w_uk, w_uv, cache)
+
+
+def choose(*arrays):
+    probe, w_uk, cache = arrays[0], arrays[3], arrays[5]
+    F, G = lax.axis_size("fsdp"), lax.axis_size("head")
+    own = w_uk.shape[1] // NOPE // F
+    fits = own > 0 and w_uk.shape[1] == own * NOPE * F and F % 2 == 0
+    fits = fits and probe.shape[1] == G and cache.shape[0] == 1
+    fits = fits and (probe.shape[0] * own) % 8 == 0 and (probe.shape[0] * G) % 8 == 0
+    fits = fits and w_uk.shape[0] % 16 == 0 and (own * R) % 128 == 0
+    return one_kernel(*arrays) if fits else per_device(*arrays)
+
+
 def solution(mesh):
     in_specs = (
         P(None, "fsdp", None),
@@ -99,5 +453,5 @@
     )
     out_specs = P(None, "fsdp", "head")
     return jax.shard_map(
-        per_device, mesh=mesh, in_specs=in_specs, out_specs=out_specs, check_vma=False
-    )
+        choose, mesh=mesh, in_specs=in_specs, out_specs=out_specs, check_vma=False
+    )

time: 318 us -> 68.2 us (0.21)
  waiting for transfers between devices: 225 us -> 0 us
  Pallas kernels: 0 us -> 61 us
  matrix products: 33.8 us -> 0 us
  local copies, waits for them, and re-layouts: 33.4 us -> 5.19 us
  between operations: 13.9 us -> 0.87 us
  starting transfers between devices: 8.33 us -> 0 us
    all_gather x4 -> x0, waiting for transfers between devices: 218 us -> none  [the longest x1 113 us: per_device(): slab = lax.all_gather(w_uq, 'fsdp', axis=0, tiled=True)]
    pallas_call x0 -> x1, Pallas kernels: none -> 61 us  [one_kernel(): pl.pallas_call(functools.partial(fused, F, G, steps, own), out_shape=jax....]
    dot_general x7 -> x0, matrix products: 33.8 us -> none  [the longest x1 25 us: per_device(): jnp.einsum('qr,hrc->qhc', flattened, absorbed, preferred_element_type=jnp...]
    all_gather x3 -> x0, local copies, waits for them, and re-layouts: 29.7 us -> none  [the longest x1 16.8 us: per_device(): slab = lax.all_gather(w_uq, 'fsdp', axis=0, tiled=True)]
    all_to_all x2 -> x0, starting transfers between devices: 8.21 us -> none  [the longest x1 4.53 us: per_device(): lax.all_to_all(mixed, 'head', split_axis=2, concat_axis=1, tiled=True)]
    unnamed x5 -> x15, local copies, waits for them, and re-layouts: 0.08 us -> 5.19 us
    all_to_all x2 -> x0, waiting for transfers between devices: 4.3 us -> none  [the longest x1 4.3 us: per_device(): lax.all_to_all(query_matrix, 'head', split_axis=1, concat_axis=2, tiled=T...]
  transfers between devices with their start and end apart: 6 -> 0, of which waited for: 4 -> 0; matrix products, arithmetic and copies ran while one was open for 20% -> 0% of each run, Pallas kernels for 0% -> 0%
where the time goes in v1:
time: 68.2 us; the launch traced here: 67.1 us
  Pallas kernels  61 us (89%)
  local copies, waits for them, and re-layouts  5.19 us (8%)
  between operations  0.87 us (1%)
    pallas_call x1, Pallas kernels, one_kernel(): pl.pallas_call(functools.partial(fused, F, G, steps, own), out_shape=jax....  61 us
    unnamed x15, local copies, waits for them, and re-layouts  5.19 us

profile of v1, /device:TPU:7, one launch (start us, length us, event | category | flops | bytes accessed | tf_op | source)
XLA Modules:
  0.0 67.1 jit_solution(163433655661184520)
XLA Ops:
  0.0 0.0 copy-start.5
  0.0 0.0 copy-start.2
  0.0 0.0 copy-start
  0.0 0.0 copy-start.4
  0.8 0.7 %copy.10.new_ref = bf16[2,1,576]{2,1,0:T(2,128)(2,1)S(1)} copy(bf16[2,1,576]{2,0,1:T(2,128)(2,1)} %param.15) | data formatting | bytes 4608 | tf_op args[6]
  1.5 1.7 %copy.11.cache_hbm = bf16[1,1024,576]{2,1,0:T(8,128)(2,1)S(1)} copy(bf16[1,1024,576]{1,2,0:T(8,128)(2,1)} %param.14) | data formatting | bytes 2359296 | tf_op args[5]
  3.2 0.0 copy-done.5
  3.2 0.0 copy-done.2
  3.2 0.0 copy-done
  3.2 0.0 copy-done.4
  3.2 0.0 copy-start.1
  3.2 1.1 %copy-done.1 = bf16[192,2048]{1,0:T(8,128)(2,1)S(1)} copy-done((bf16[192,2048]{1,0:T(8,128)(2,1)S(1)}, bf16[192,2048]{1,0:T(8,128)(2,1)}, u32[]{:S(2)}) %copy-start.1) | copy-done | bytes 786456
  4.4 0.0 copy-start.3
  4.4 1.0 %copy-done.3 = bf16[64,4096]{1,0:T(8,128)(2,1)S(1)} copy-done((bf16[64,4096]{1,0:T(8,128)(2,1)S(1)}, bf16[64,4096]{1,0:T(8,128)(2,1)}, u32[]{:S(2)}) %copy-start.3) | copy-done | bytes 524312
  5.4 61.0 %shard_map.91 = bf16[2,4,4096]{2,1,0:T(4,128)(2,1)S(1)} custom-call(s32[1]{0:T(128)S(6)} %copy.13.len_ref, f32[1,128]{1,0:T(1,128)S(1)} %copy-done.5, bf16[2,4,1536]{2,1,0:T(4,128)(2,1)S(1)} %copy-done.4, bf16[2,1,576]{2,1,0:T(2,128)(2,1)S(1)} %copy.10.new_ref, bf16[192,4096]{1,0:T(8,128)(2,1)S(1)} %copy-done, bf16[192,2048]{1,0:T(8,128)(2,1)S(1)} %copy-done.1, ...), custom_call_target="tpu_custom_call" | custom-call | tf_op jit(solution)/shard_map/pallas_call | solution.py:411
  66.5 0.6 copy.14
Async XLA Ops:
  0.0 3.2 %copy-start.5 = (f32[1,128]{1,0:T(1,128)S(1)}, f32[1,128]{1,0:T(1,128)}, u32[]{:S(2)}) copy-start(f32[1,128]{1,0:T(1,128)} %constant.2.clone.freq_ref) | copy-start | bytes 1540
  0.0 3.2 %copy-start.2 = (bf16[64,4096]{1,0:T(8,128)(2,1)S(1)}, bf16[64,4096]{1,0:T(8,128)(2,1)}, u32[]{:S(2)}) copy-start(bf16[64,4096]{1,0:T(8,128)(2,1)} %uk_hbm.1) | copy-start | bytes 1572868
  0.0 3.2 %copy-start = (bf16[192,4096]{1,0:T(8,128)(2,1)S(1)}, bf16[192,4096]{1,0:T(8,128)(2,1)}, u32[]{:S(2)}) copy-start(bf16[192,4096]{1,0:T(8,128)(2,1)} %uq_hbm.1) | copy-start | bytes 4718596
  0.0 3.2 %copy-start.4 = (bf16[2,4,1536]{2,1,0:T(4,128)(2,1)S(1)}, bf16[2,4,1536]{2,1,0:T(4,128)(2,1)}, u32[]{:S(2)}) copy-start(bf16[2,4,1536]{2,1,0:T(4,128)(2,1)} %probe_ref.1) | copy-start | bytes 73732
  3.2 1.1 %copy-start.1 = (bf16[192,2048]{1,0:T(8,128)(2,1)S(1)}, bf16[192,2048]{1,0:T(8,128)(2,1)}, u32[]{:S(2)}) copy-start(bf16[192,2048]{1,0:T(8,128)(2,1)} %qr_hbm.1) | copy-start | bytes 2359300
  4.4 1.0 %copy-start.3 = (bf16[64,4096]{1,0:T(8,128)(2,1)S(1)}, bf16[64,4096]{1,0:T(8,128)(2,1)}, u32[]{:S(2)}) copy-start(bf16[64,4096]{1,0:T(8,128)(2,1)} %uv_hbm.1) | copy-start | bytes 1572868

commit v2 on v1

--- a/solution.py
+++ b/solution.py
@@ -92,10 +92,11 @@
 
 
 def fused(F, G, steps, own,
-          len_ref, freq_ref, probe_ref, new_ref, uq_hbm, qr_hbm, uk_hbm, uv_hbm, cache_hbm,
+          len_ref, freq_hbm, probe_hbm, new_hbm, uq_hbm, qr_hbm, uk_hbm, uv_hbm, cache_hbm,
           out_ref,
-          uq, wqr, wk, wv, kv, ps, pr, pp, pv, zs, zr, qs, qr, ms, mr, os_, or_,
-          lsem, sp, rp, sk, rk, sv, rv, spp, rpp, sz, rz, sq, rq, sm, rm, so, ro):
+          freq_ref, probe_ref, new_ref,
+          uq, wqr, wk, wv, kv, ps, pr, pp, pv, zs, zr, nq, es_, er_, qs, qr, ms, mr, vs, vr,
+          lsem, sp, rp, sk, rk, spp, rpp, sz, rz, sn, rn, se, re_, sq, rq, sm, rm, so, ro):
     f32, bf16 = jnp.float32, jnp.bfloat16
     f = lax.axis_index("fsdp")
     hd = lax.axis_index("head")
@@ -107,7 +108,7 @@
     cols = own * NOPE
     rcols = own * R
     C = ck * F
-    stored = cache_hbm.shape[1]
+    stored = cache_hbm.shape[2]
     slice_rank = uq.shape[0]
     per = steps * own
     queries = F * steps * G
@@ -122,13 +123,17 @@
     def block(t, width):
         return pl.ds(pl.multiple_of(t * width, 128), width)
 
-    mine = pl.ds(pl.multiple_of(f * ck, 16), ck)
+    hcols = Z * cols
+    mine = pl.ds(pl.multiple_of(core * ck, 16), ck)
     load_uq = pltpu.make_async_copy(uq_hbm, uq, lsem.at[0])
     load_qr = pltpu.make_async_copy(qr_hbm, wqr, lsem.at[1])
-    load_kv = pltpu.make_async_copy(cache_hbm.at[0], kv.at[pl.ds(0, stored)], lsem.at[2])
-    load_uk = pltpu.make_async_copy(uk_hbm.at[:, block(f, cols)], wk.at[mine], lsem.at[3])
-    load_uv = pltpu.make_async_copy(uv_hbm.at[:, block(f, cols)], wv.at[mine], lsem.at[4])
-    loads = [load_uq, load_qr, load_kv, load_uk, load_uv]
+    load_kv = pltpu.make_async_copy(cache_hbm.at[0], kv, lsem.at[2])
+    load_uk = pltpu.make_async_copy(uk_hbm.at[:, block(core, hcols)], wk.at[mine], lsem.at[3])
+    load_uv = pltpu.make_async_copy(uv_hbm.at[:, block(core, hcols)], wv.at[mine], lsem.at[4])
+    load_probe = pltpu.make_async_copy(probe_hbm, probe_ref, lsem.at[5])
+    load_new = pltpu.make_async_copy(new_hbm, new_ref, lsem.at[6])
+    load_freq = pltpu.make_async_copy(freq_hbm, freq_ref, lsem.at[7])
+    loads = [load_probe, load_uq, load_qr, load_new, load_freq, load_uk, load_kv, load_uv]
     for c in loads:
         c.start()
 
@@ -144,6 +149,7 @@
 
     lax.fori_loop(1, N, greet, 0)
 
+    load_probe.wait()
     probe8 = jnp.concatenate([probe_ref[s].astype(f32) for s in range(steps)], axis=0)
     for p in range(F):
         ps[p] = probe8[:, p * slice_rank:(p + 1) * slice_rank].astype(bf16)
@@ -155,13 +161,9 @@
         t = lax.rem(f + k, F)
         return rcopy(ps.at[t], pr.at[f], sp.at[k], rp.at[f], t, hd)
 
-    def uk_copy(k):
-        t = lax.rem(f + k, F)
-        return rcopy(uk_hbm.at[:, block(t, cols)], wk.at[mine], sk.at[k], rk.at[f], t, hd)
-
-    def uv_copy(k):
-        t = lax.rem(f + k, F)
-        return rcopy(uv_hbm.at[:, block(t, cols)], wv.at[mine], sv.at[k], rv.at[f], t, hd)
+    def weight_copy(i):
+        hbm, w = ((uk_hbm, wk), (uv_hbm, wv))[i]
+        return rcopy(hbm.at[:, block(1 - core, hcols)], w.at[mine], sk.at[i], rk.at[i], z * 2 + 1 - core, hd)
 
     def each(first, last, make, method):
         def step(k, carry):
@@ -170,14 +172,16 @@
         lax.fori_loop(first, last, step, 0)
 
     each(1, F, probe_copy, "start")
-    each(1, F, uk_copy, "start")
-
-    tail = kv.shape[0] - stored
-    at = lax.broadcasted_iota(jnp.int32, (tail, kv.shape[1]), 0)
-    fill = jnp.zeros((tail, kv.shape[1]), f32)
+    weight_copy(0).start()
+    weight_copy(1).start()
+
+    load_new.wait()
+    load_freq.wait()
+    at = lax.broadcasted_iota(jnp.int32, (128, C + R), 0)
+    fill = jnp.zeros((128, C + R), f32)
     for s in range(steps):
-        fill = jnp.where(at == s, new_ref[s].astype(f32), fill)
-    kv[stored:stored + tail, :] = fill.astype(bf16)
+        fill = jnp.where(at == s, new_ref[0, s:s + 1].astype(f32), fill)
+    fresh = fill.astype(bf16)
 
     row8 = lax.broadcasted_iota(jnp.int32, (per, 128), 0)
     step8 = lax.div(row8, own)
@@ -206,7 +210,7 @@
 
     def to_partner(k, carry):
         zz = lax.rem(z + k, Z)
-        a, b = partial_of(zz * 2 + 1 - core)
+        a, b = partial_of((1 - core) * Z + zz)
         pp[zz, :, 0:cols] = a.astype(bf16)
         pp[zz, :, cols:cols + rcols] = b.astype(bf16)
         pair_copy(k).start()
@@ -220,7 +224,7 @@
 
     def along_line(k, carry):
         zz = lax.rem(z + k, Z)
-        a, b = partial_of(zz * 2 + core)
+        a, b = partial_of(core * Z + zz)
         pair_copy(k).wait_recv()
         zs[zz, :, 0:cols] = (a + pv[zz, :, 0:cols].astype(f32)).astype(bf16)
         zs[zz, :, cols:cols + rcols] = (b + pv[zz, :, cols:cols + rcols].astype(f32)).astype(bf16)
@@ -228,7 +232,7 @@
         return carry
 
     lax.fori_loop(1, Z, along_line, 0)
-    a, b = partial_of(f)
+    a, b = partial_of(core * Z + z)
     pair_copy(0).wait_recv()
     nope = a + pv[z, :, 0:cols].astype(f32)
     rope = b + pv[z, :, cols:cols + rcols].astype(f32)
@@ -237,8 +241,14 @@
         rcopy(zs.at[src], zr.at[src], sz.at[src], rz.at[src], src * 2 + core, hd).wait_recv()
         nope = nope + zr[src, :, 0:cols].astype(f32)
         rope = rope + zr[src, :, cols:cols + rcols].astype(f32)
-    nope = nope.astype(bf16)
+    nq[pl.ds(z, 1)] = nope.astype(bf16).reshape(1, queries, cols)
     rope = rope.astype(bf16)
+
+    def nope_copy(k):
+        zz = lax.rem(z + k, Z)
+        return rcopy(nq.at[z], nq.at[z], sn.at[k], rn.at[z], zz * 2 + core, hd)
+
+    each(1, Z, nope_copy, "start")
 
     def iota(shape, axis):
         return lax.broadcasted_iota(jnp.int32, shape, axis)
@@ -253,36 +263,53 @@
     own_rope = lax.div(iota((expanded, rcols), 1), R) == lax.rem(iota((expanded, rcols), 0), own)
     fold = lax.rem(iota((rcols, 128), 0), R) == iota((rcols, 128), 1)
     fold = jnp.where(fold, 1.0, 0.0).astype(bf16)
-    wide = jnp.where(own_head, jnp.dot(pick, nope, preferred_element_type=f32), 0.0).astype(bf16)
     wide_rope = jnp.where(own_rope, jnp.dot(pick, rope, preferred_element_type=f32), 0.0).astype(bf16)
     rope_rows = jnp.dot(wide_rope, fold, preferred_element_type=f32)
+    es_[...] = rope_rows.reshape(N, per, 128).astype(bf16)
+    part = hd * 2 + core
+    slot = part * Z + z
+
+    def rope_copy(k):
+        t = lax.rem(me + k, N)
+        return rcopy(es_.at[t], er_.at[slot], se.at[k], re_.at[slot], lax.div(t, G), lax.rem(t, G))
+
+    each(1, N, rope_copy, "start")
+    er_[pl.ds(slot, 1)] = es_[pl.ds(me, 1)]
 
     load_uk.wait()
-
-    def weight_arrival(hbm, w, ssem, rsem):
-        def step(k, carry):
-            src = lax.rem(f + k, F)
-            there = pl.ds(pl.multiple_of(src * ck, 16), ck)
-            rcopy(hbm.at[:, block(src, cols)], w.at[there], ssem.at[k], rsem.at[src], src, hd).wait_recv()
-            return carry
-        lax.fori_loop(1, F, step, 0)
-
-    weight_arrival(uk_hbm, wk, sk, rk)
-    latent = lax.dot_general(wide, wk[...], (((1,), (1,)), ((), ())), preferred_element_type=f32)
-    qs[:, :, 0:C] = latent.reshape(N, per, C).astype(bf16)
-    qs[:, :, C:C + 128] = rope_rows.reshape(N, per, 128).astype(bf16)
+    theirs = pl.ds(pl.multiple_of((1 - core) * ck, 16), ck)
+
+    def weight_arrival(i):
+        hbm, w = ((uk_hbm, wk), (uv_hbm, wv))[i]
+        rcopy(hbm.at[:, block(core, hcols)], w.at[theirs], sk.at[i], rk.at[i], z * 2 + 1 - core, hd).wait_recv()
+
+    weight_arrival(0)
+    for k in range(1, Z):
+        src = lax.rem(z + k, Z)
+        rcopy(nq.at[src], nq.at[src], sn.at[k], rn.at[src], src * 2 + core, hd).wait_recv()
+    for h in range(Z):
+        wide = jnp.where(own_head, jnp.dot(pick, nq[h], preferred_element_type=f32), 0.0).astype(bf16)
+        latent = lax.dot_general(
+            wide, wk[:, h * cols:(h + 1) * cols], (((1,), (1,)), ((), ())), preferred_element_type=f32
+        )
+        qs[:, h * per:(h + 1) * per, :] = latent.reshape(N, per, 2 * ck).astype(bf16)
+
+    tall = Z * per
+
+    def tile(p, zz):
+        return (pl.ds(pl.multiple_of(p * tall, 16), tall), pl.ds(pl.multiple_of(zz * 2 * ck, 128), 2 * ck))
 
     def query_copy(k):
         t = lax.rem(me + k, N)
-        return rcopy(qs.at[t], qr.at[me], sq.at[k], rq.at[me], lax.div(t, G), lax.rem(t, G))
+        return rcopy(qs.at[t], qr.at[tile(part, z)], sq.at[k], rq.at[slot], lax.div(t, G), lax.rem(t, G))
 
     each(1, N, query_copy, "start")
-    each(1, F, uv_copy, "start")
-    qr[pl.ds(me, 1)] = qs[pl.ds(me, 1)]
+    qr[tile(part, z)] = qs[pl.ds(me, 1)].reshape(tall, 2 * ck)
 
     load_kv.wait()
     factor = (NOPE + R) ** -0.5
     chunk = F
+    keys = stored + 128
     sr = iota((128, 128), 0)
     sc = iota((128, 128), 1)
     half = R // 2
@@ -290,100 +317,108 @@
     swap = swap + jnp.where((sr == sc - half) & (sc >= half) & (sc < R), 1.0, 0.0)
     swap = swap.astype(bf16)
     rows = chunk * per
-    keys = kv.shape[0]
     cosines = jnp.broadcast_to(cos8[None], (chunk, per, 128)).reshape(rows, 128)
     sines = jnp.broadcast_to(sin8[None], (chunk, per, 128)).reshape(rows, 128)
     column = iota((rows, keys), 1)
     step_of = lax.div(lax.rem(iota((rows, keys), 0), per), own)
     shown = (column < len_ref[0]) | ((column >= stored) & (column <= stored + step_of))
 
-    def mixed_copy(e):
-        return rcopy(ms.at[e], mr.at[me], sm.at[e], rm.at[me], lax.div(e, G), lax.rem(e, G))
+    def mixed_copy(b, i):
+        zz, cc = lax.div(i, 2), lax.rem(i, 2)
+        e = i * G + b
+        return rcopy(ms.at[tile(b * 2 + cc, zz)], mr.at[me], sm.at[e], rm.at[me], i, b)
 
     def attend_chunk(b, carry):
-        base = b * chunk
-
         def arrival(i, c):
-            src = base + i
-
-            @pl.when(src != me)
+            zz, cc = lax.div(i, 2), lax.rem(i, 2)
+            at_slot = (b * 2 + cc) * Z + zz
+
+            @pl.when(i * G + b != me)
             def _():
-                rcopy(qs.at[src], qr.at[src], sq.at[0], rq.at[src], lax.div(src, G), lax.rem(src, G)).wait_recv()
+                rcopy(es_.at[0], er_.at[at_slot], se.at[0], re_.at[at_slot], i, b).wait_recv()
+                rcopy(qs.at[0], qr.at[tile(b * 2 + cc, zz)], sq.at[0], rq.at[at_slot], i, b).wait_recv()
             return c
 
         lax.fori_loop(0, chunk, arrival, 0)
-        x = qr[pl.ds(base, chunk)].astype(f32).reshape(rows, C + 128)
-        lat = x[:, 0:C].astype(bf16)
-        xr = x[:, C:C + 128]
+        here = pl.ds(pl.multiple_of(b * rows, 16), rows)
+        lat = qr[here, :]
+        xr = er_[pl.ds(b * chunk, chunk)].astype(f32).reshape(rows, 128)
         turned = jnp.dot(xr.astype(bf16), swap, preferred_element_type=f32)
         rot = (xr * cosines + turned * sines).astype(bf16)[:, 0:R]
         nt = (((1,), (1,)), ((), ()))
-        s = lax.dot_general(lat, kv[:, 0:C], nt, preferred_element_type=f32)
-        s = s + lax.dot_general(rot, kv[:, C:C + R], nt, preferred_element_type=f32)
+        s = jnp.dot(lat, kv[0:C, :], preferred_element_type=f32)
+        s = s + jnp.dot(rot, kv[C:C + R, :], preferred_element_type=f32)
+        n = lax.dot_general(lat, fresh[:, 0:C], nt, preferred_element_type=f32)
+        n = n + lax.dot_general(rot, fresh[:, C:C + R], nt, preferred_element_type=f32)
+        s = jnp.concatenate([s, n], axis=1)
         s = jnp.where(shown, s * factor, -1e30)
         m = jnp.max(s, axis=1, keepdims=True)
         w = jnp.exp(s - m)
         total = jnp.sum(w, axis=1, keepdims=True)
-        mix = jnp.dot(w.astype(bf16), kv[:, 0:C], preferred_element_type=f32) / total
-        ms[pl.ds(base, chunk)] = mix.reshape(chunk, per, C).astype(bf16)
+        w = w.astype(bf16)
+        mix = lax.dot_general(w[:, 0:stored], kv[0:C, :], nt, preferred_element_type=f32)
+        mix = mix + jnp.dot(w[:, stored:], fresh[:, 0:C], preferred_element_type=f32)
+        ms[here, :] = (mix / total).astype(bf16)
 
         def send(i, c):
-            e = base + i
-
-            @pl.when(e != me)
+            @pl.when(i * G + b != me)
             def _():
-                mixed_copy(e).start()
+                mixed_copy(b, i).start()
             return c
 
         lax.fori_loop(0, chunk, send, 0)
         return carry
 
-    lax.fori_loop(0, N // chunk, attend_chunk, 0)
-    mr[pl.ds(me, 1)] = ms[pl.ds(me, 1)]
+    lax.fori_loop(0, G, attend_chunk, 0)
+    mr[pl.ds(me, 1)] = ms[tile(part, z)].reshape(1, tall, 2 * ck)
 
     load_uv.wait()
-    weight_arrival(uv_hbm, wv, sv, rv)
+    weight_arrival(1)
 
     def mixed_arrival(k, carry):
         src = lax.rem(me + k, N)
-        rcopy(ms.at[src], mr.at[src], sm.at[src], rm.at[src], lax.div(src, G), lax.rem(src, G)).wait_recv()
+        rcopy(ms.at[tile(0, 0)], mr.at[src], sm.at[src], rm.at[src], lax.div(src, G), lax.rem(src, G)).wait_recv()
         return carry
 
     lax.fori_loop(1, N, mixed_arrival, 0)
-    mixed = mr[...].astype(f32).reshape(expanded, C).astype(bf16)
-    values = jnp.dot(mixed, wv[...], preferred_element_type=f32)
-    values = jnp.where(own_head, values, 0.0).astype(bf16)
-    values = lax.dot_general(pick, values, (((0,), (0,)), ((), ())), preferred_element_type=f32)
-    os_[...] = values.reshape(F, steps * G, cols).astype(bf16)
+    for h in range(Z):
+        mixed = mr[:, h * per:(h + 1) * per, :].astype(f32).reshape(expanded, 2 * ck).astype(bf16)
+        values = jnp.dot(mixed, wv[:, h * cols:(h + 1) * cols], preferred_element_type=f32)
+        values = jnp.where(own_head, values, 0.0).astype(bf16)
+        values = lax.dot_general(pick, values, (((0,), (0,)), ((), ())), preferred_element_type=f32)
+        vs[:, :, h * cols:(h + 1) * cols] = values.reshape(F, steps * G, cols).astype(bf16)
 
     def out_copy(k):
         t = lax.rem(f + k, F)
-        return rcopy(os_.at[t], or_.at[f], so.at[k], ro.at[f], t, hd)
+        return rcopy(vs.at[t], vr.at[f], so.at[k], ro.at[f], t, hd)
 
     each(1, F, out_copy, "start")
-    or_[pl.ds(f, 1)] = os_[pl.ds(f, 1)]
+    vr[pl.ds(f, 1)] = vs[pl.ds(f, 1)]
 
     def out_arrival(k, carry):
         src = lax.rem(f + k, F)
-        rcopy(os_.at[src], or_.at[src], so.at[k], ro.at[src], src, hd).wait_recv()
+        rcopy(vs.at[src], vr.at[src], so.at[k], ro.at[src], src, hd).wait_recv()
         return carry
 
     lax.fori_loop(1, F, out_arrival, 0)
-    for p in range(F):
-        v = or_[p].astype(f32)
+    for p in range(2):
+        v = sum(vr[zz * 2 + p].astype(f32) for zz in range(Z))
         for s in range(steps):
-            out_ref[s, :, p * cols:(p + 1) * cols] = v[s * G:(s + 1) * G].astype(bf16)
+            out_ref[s, :, p * hcols:(p + 1) * hcols] = v[s * G:(s + 1) * G].astype(bf16)
 
     each(1, F, probe_copy, "wait_send")
-    each(1, F, uk_copy, "wait_send")
-    each(1, F, uv_copy, "wait_send")
+    weight_copy(0).wait_send()
+    weight_copy(1).wait_send()
+    each(1, Z, nope_copy, "wait_send")
+    each(1, N, rope_copy, "wait_send")
     each(1, Z + 1, pair_copy, "wait_send")
     each(1, Z, line_copy, "wait_send")
     each(1, N, query_copy, "wait_send")
     each(1, F, out_copy, "wait_send")
 
     def mixed_sent(k, carry):
-        mixed_copy(lax.rem(me + k, N)).wait_send()
+        t = lax.rem(me + k, N)
+        mixed_copy(lax.rem(t, G), lax.div(t, G)).wait_send()
         return carry
 
     lax.fori_loop(1, N, mixed_sent, 0)
@@ -399,7 +434,9 @@
     queries = F * steps * G
     per = steps * own
     cols, rcols = own * NOPE, own * R
-    stored, width = cache.shape[1:]
+    hcols = Z * cols
+    cache = cache.transpose(0, 2, 1)
+    new_kv = new_kv.transpose(1, 0, 2)
     half = R // 2
     freqs = 10000.0 ** (-(np.arange(half, dtype=np.float32) * 2.0 / R))
     freqs = np.concatenate([freqs, freqs, np.zeros(128 - R)]).astype(np.float32)[None]
@@ -407,21 +444,23 @@
     vm = lambda *shape: pltpu.VMEM(shape, bf16)
     dma = lambda n: pltpu.SemaphoreType.DMA((n,))
     vmem = pl.BlockSpec(memory_space=pltpu.VMEM)
-    hbm = pl.BlockSpec(memory_space=pl.ANY)
+    hbm = pl.BlockSpec(memory_space=pltpu.HBM)
     return pl.pallas_call(
         functools.partial(fused, F, G, steps, own),
         out_shape=jax.ShapeDtypeStruct((steps, group, heads * VDIM), bf16),
-        in_specs=[pl.BlockSpec(memory_space=pltpu.SMEM), vmem, vmem, vmem, hbm, hbm, hbm, hbm, hbm],
+        in_specs=[pl.BlockSpec(memory_space=pltpu.SMEM)] + [hbm] * 8,
         out_specs=vmem,
         scratch_shapes=[
-            vm(*w_uq.shape), vm(*w_qr.shape), vm(C, cols), vm(C, cols), vm(stored + 128, width),
+            pltpu.VMEM((1, 128), jnp.float32), vm(*probe_compressed.shape), vm(*new_kv.shape),
+            vm(*w_uq.shape), vm(*w_qr.shape), vm(2 * ck, hcols), vm(2 * ck, hcols), vm(*cache.shape[1:]),
             vm(F, steps * G, w_uq.shape[0]), vm(F, steps * G, w_uq.shape[0]),
             vm(Z, queries, cols + rcols), vm(Z, queries, cols + rcols),
             vm(Z, queries, cols + rcols), vm(Z, queries, cols + rcols),
-            vm(N, per, C + 128), vm(N, per, C + 128), vm(N, per, C), vm(N, per, C),
-            vm(F, steps * G, cols), vm(F, steps * G, cols),
-            dma(5), dma(F), dma(F), dma(F), dma(F), dma(F), dma(F), dma(Z), dma(Z), dma(Z), dma(Z),
-            dma(N), dma(N), dma(N), dma(N), dma(F), dma(F),
+            vm(Z, queries, cols), vm(N, per, 128), vm(N, per, 128),
+            vm(N, Z * per, 2 * ck), vm(2 * G * Z * per, C), vm(2 * G * Z * per, C), vm(N, Z * per, 2 * ck),
+            vm(F, steps * G, hcols), vm(F, steps * G, hcols),
+            dma(8), dma(F), dma(F), dma(2), dma(2), dma(Z), dma(Z), dma(Z), dma(Z), dma(Z), dma(Z),
+            dma(N), dma(N), dma(N), dma(N), dma(N), dma(N), dma(F), dma(F),
         ],
         compiler_params=pltpu.CompilerParams(
             collective_id=0, has_side_effects=True, vmem_limit_bytes=48 * 2**20
@@ -436,7 +475,7 @@
     fits = own > 0 and w_uk.shape[1] == own * NOPE * F and F % 2 == 0
     fits = fits and probe.shape[1] == G and cache.shape[0] == 1
     fits = fits and (probe.shape[0] * own) % 8 == 0 and (probe.shape[0] * G) % 8 == 0
-    fits = fits and w_uk.shape[0] % 16 == 0 and (own * R) % 128 == 0
+    fits = fits and w_uk.shape[0] % 16 == 0 and (2 * w_uk.shape[0]) % 128 == 0 and cache.shape[1] % 128 == 0 and (own * R) % 128 == 0
     return one_kernel(*arrays) if fits else per_device(*arrays)
 
 

time: 68.2 us -> 65.8 us (0.965)
  Pallas kernels: 61 us -> 56.1 us
  local copies, waits for them, and re-layouts: 5.19 us -> 8.59 us
    pallas_call x1, Pallas kernels: 61 us -> 56.1 us  [one_kernel(): pl.pallas_call(functools.partial(fused, F, G, steps, own), out_shape=jax....]
    unnamed x15 -> x17, local copies, waits for them, and re-layouts: 5.19 us -> 8.59 us
where the time goes in v2:
time: 65.8 us; the launch traced here: 65.3 us
  Pallas kernels  56.1 us (85%)
  local copies, waits for them, and re-layouts  8.59 us (13%)
  between operations  0.68 us (1%)
    pallas_call x1, Pallas kernels, one_kernel(): pl.pallas_call(functools.partial(fused, F, G, steps, own), out_shape=jax....  56.1 us
    unnamed x17, local copies, waits for them, and re-layouts  8.59 us

profile of v2, /device:TPU:7, one launch (start us, length us, event | category | flops | bytes accessed | tf_op | source)
XLA Modules:
  0.0 65.3 jit_solution(11108455228370592677)
XLA Ops:
  0.7 0.0 copy-start
  0.7 1.4 %copy-done = bf16[192,4096]{1,0:T(8,128)(2,1)S(1)} copy-done((bf16[192,4096]{1,0:T(8,128)(2,1)S(1)}, bf16[192,4096]{1,0:T(8,128)(2,1)}, u32[]{:S(2)}) %copy-start) | copy-done | bytes 1572888
  2.1 0.0 copy-start.1
  2.1 1.3 %copy-done.1 = bf16[1,1024,576]{1,2,0:T(8,128)(2,1)S(1)} copy-done((bf16[1,1024,576]{1,2,0:T(8,128)(2,1)S(1)}, bf16[1,1024,576]{1,2,0:T(8,128)(2,1)}, u32[]{:S(2)}) %copy-start.1) | copy-done | bytes 1179672
  3.3 0.0 copy-start.2
  3.3 1.1 %copy-done.2 = bf16[192,2048]{1,0:T(8,128)(2,1)S(1)} copy-done((bf16[192,2048]{1,0:T(8,128)(2,1)S(1)}, bf16[192,2048]{1,0:T(8,128)(2,1)}, u32[]{:S(2)}) %copy-start.2) | copy-done | bytes 786456
  4.5 0.0 copy-start.3
  4.5 1.0 %copy-done.3 = bf16[64,4096]{1,0:T(8,128)(2,1)S(1)} copy-done((bf16[64,4096]{1,0:T(8,128)(2,1)S(1)}, bf16[64,4096]{1,0:T(8,128)(2,1)}, u32[]{:S(2)}) %copy-start.3) | copy-done | bytes 524312
  5.5 0.0 copy-start.4
  5.5 1.0 %copy-done.4 = bf16[64,4096]{1,0:T(8,128)(2,1)S(1)} copy-done((bf16[64,4096]{1,0:T(8,128)(2,1)S(1)}, bf16[64,4096]{1,0:T(8,128)(2,1)}, u32[]{:S(2)}) %copy-start.4) | copy-done | bytes 524312
  6.5 0.0 copy-start.5
  6.6 0.7 %copy-done.5 = bf16[2,4,1536]{2,1,0:T(4,128)(2,1)S(1)} copy-done((bf16[2,4,1536]{2,1,0:T(4,128)(2,1)S(1)}, bf16[2,4,1536]{2,1,0:T(4,128)(2,1)}, u32[]{:S(2)}) %copy-start.5) | copy-done | bytes 24600
  7.3 0.0 copy-start.6
  7.3 0.7 %copy-done.6 = bf16[2,1,576]{2,0,1:T(2,128)(2,1)S(1)} copy-done((bf16[2,1,576]{2,0,1:T(2,128)(2,1)S(1)}, bf16[2,1,576]{2,0,1:T(2,128)(2,1)}, u32[]{:S(2)}) %copy-start.6) | copy-done | bytes 2328
  8.0 0.0 copy-start.7
  8.0 0.7 copy-done.7
  8.6 56.1 %shard_map.91 = bf16[2,4,4096]{2,1,0:T(4,128)(2,1)S(1)} custom-call(s32[1]{0:T(128)S(6)} %copy.11.len_ref, f32[1,128]{1,0:T(1,128)S(1)} %copy-done.7, bf16[2,4,1536]{2,1,0:T(4,128)(2,1)S(1)} %copy-done.5, bf16[1,2,576]{2,1,0:T(2,128)(2,1)S(1)} %bitcast.3, bf16[192,4096]{1,0:T(8,128)(2,1)S(1)} %copy-done, bf16[192,2048]{1,0:T(8,128)(2,1)S(1)} %copy-done.2, ...), custom_call_target="tpu_custom_call" | custom-call | tf_op jit(solution)/shard_map/pallas_call | solution.py:448
  64.7 0.6 copy.12
Async XLA Ops:
  0.7 1.4 %copy-start = (bf16[192,4096]{1,0:T(8,128)(2,1)S(1)}, bf16[192,4096]{1,0:T(8,128)(2,1)}, u32[]{:S(2)}) copy-start(bf16[192,4096]{1,0:T(8,128)(2,1)} %uq_hbm.1) | copy-start | bytes 4718596
  2.1 1.3 %copy-start.1 = (bf16[1,1024,576]{1,2,0:T(8,128)(2,1)S(1)}, bf16[1,1024,576]{1,2,0:T(8,128)(2,1)}, u32[]{:S(2)}) copy-start(bf16[1,1024,576]{1,2,0:T(8,128)(2,1)} %param.14) | copy-start | bytes 3538948
  3.3 1.1 %copy-start.2 = (bf16[192,2048]{1,0:T(8,128)(2,1)S(1)}, bf16[192,2048]{1,0:T(8,128)(2,1)}, u32[]{:S(2)}) copy-start(bf16[192,2048]{1,0:T(8,128)(2,1)} %qr_hbm.1) | copy-start | bytes 2359300
  4.5 1.0 %copy-start.3 = (bf16[64,4096]{1,0:T(8,128)(2,1)S(1)}, bf16[64,4096]{1,0:T(8,128)(2,1)}, u32[]{:S(2)}) copy-start(bf16[64,4096]{1,0:T(8,128)(2,1)} %uk_hbm.1) | copy-start | bytes 1572868
  5.5 1.0 %copy-start.4 = (bf16[64,4096]{1,0:T(8,128)(2,1)S(1)}, bf16[64,4096]{1,0:T(8,128)(2,1)}, u32[]{:S(2)}) copy-start(bf16[64,4096]{1,0:T(8,128)(2,1)} %uv_hbm.1) | copy-start | bytes 1572868
  6.5 0.7 %copy-start.5 = (bf16[2,4,1536]{2,1,0:T(4,128)(2,1)S(1)}, bf16[2,4,1536]{2,1,0:T(4,128)(2,1)}, u32[]{:S(2)}) copy-start(bf16[2,4,1536]{2,1,0:T(4,128)(2,1)} %probe_hbm.1) | copy-start | bytes 73732
  7.3 0.7 %copy-start.6 = (bf16[2,1,576]{2,0,1:T(2,128)(2,1)S(1)}, bf16[2,1,576]{2,0,1:T(2,128)(2,1)}, u32[]{:S(2)}) copy-start(bf16[2,1,576]{2,0,1:T(2,128)(2,1)} %param.15) | copy-start | bytes 6916
  8.0 0.7 %copy-start.7 = (f32[1,128]{1,0:T(1,128)S(1)}, f32[1,128]{1,0:T(1,128)}, u32[]{:S(2)}) copy-start(f32[1,128]{1,0:T(1,128)} %constant.2.clone.freq_hbm) | copy-start | bytes 1540

commit v3 on v2

--- a/solution.py
+++ b/solution.py
@@ -300,8 +300,9 @@
         return (pl.ds(pl.multiple_of(p * tall, 16), tall), pl.ds(pl.multiple_of(zz * 2 * ck, 128), 2 * ck))
 
     def query_copy(k):
-        t = lax.rem(me + k, N)
-        return rcopy(qs.at[t], qr.at[tile(part, z)], sq.at[k], rq.at[slot], lax.div(t, G), lax.rem(t, G))
+        ff = lax.rem(f + lax.rem(k, F), F)
+        hh = lax.rem(hd + lax.div(k, F), G)
+        return rcopy(qs.at[ff * G + hh], qr.at[tile(part, z)], sq.at[k], rq.at[slot], ff, hh)
 
     each(1, N, query_copy, "start")
     qr[tile(part, z)] = qs[pl.ds(me, 1)].reshape(tall, 2 * ck)
@@ -328,7 +329,9 @@
         e = i * G + b
         return rcopy(ms.at[tile(b * 2 + cc, zz)], mr.at[me], sm.at[e], rm.at[me], i, b)
 
-    def attend_chunk(b, carry):
+    def attend_chunk(turn, carry):
+        b = lax.rem(hd + G - turn, G)
+
         def arrival(i, c):
             zz, cc = lax.div(i, 2), lax.rem(i, 2)
             at_slot = (b * 2 + cc) * Z + zz
@@ -463,7 +466,7 @@
             dma(N), dma(N), dma(N), dma(N), dma(N), dma(N), dma(F), dma(F),
         ],
         compiler_params=pltpu.CompilerParams(
-            collective_id=0, has_side_effects=True, vmem_limit_bytes=48 * 2**20
+            collective_id=0, has_side_effects=True, vmem_limit_bytes=67043328
         ),
     )(lengths, jnp.asarray(freqs), probe_compressed, new_kv, w_uq, w_qr, w_uk, w_uv, cache)
 

time: 65.8 us -> 58.1 us (0.88)
  the two profiles are of different devices: /device:TPU:7 before, /device:TPU:1 now
where the time goes in v3:
time: 58.1 us; the launch traced here: 57.9 us
  Pallas kernels  55.7 us (96%)
  local copies, waits for them, and re-layouts  1.49 us (3%)
  between operations  0.66 us (1%)
    pallas_call x1, Pallas kernels, one_kernel(): pl.pallas_call(functools.partial(fused, F, G, steps, own), out_shape=jax....  55.7 us
    unnamed x1, local copies, waits for them, and re-layouts  1.49 us

profile of v3, /device:TPU:1, one launch (start us, length us, event | category | flops | bytes accessed | tf_op | source)
XLA Modules:
  0.0 57.9 jit_solution(3408682826200419548)
XLA Ops:
  0.7 55.7 %shard_map.91 = bf16[2,4,4096]{2,1,0:T(4,128)(2,1)} custom-call(s32[1]{0:T(128)S(6)} %copy.11.len_ref, f32[1,128]{1,0:T(1,128)} %constant.2.clone.freq_hbm, bf16[2,4,1536]{2,1,0:T(4,128)(2,1)} %probe_hbm.1, bf16[1,2,576]{2,1,0:T(2,128)(2,1)} %bitcast.3, bf16[192,4096]{1,0:T(8,128)(2,1)} %uq_hbm.1, bf16[192,2048]{1,0:T(8,128)(2,1)} %qr_hbm.1, ...), custom_call_target="tpu_custom_call" | custom-call | tf_op jit(solution)/shard_map/pallas_call | solution.py:451
  56.4 1.5 %copy.12 = bf16[2,4,4096]{2,1,0:T(4,128)(2,1)} copy(bf16[2,4,4096]{2,1,0:T(4,128)(2,1)} %shard_map.91) | data formatting | bytes 131072
